TPU v7x, 32 devices: a whole 2x2x4 slice. The times are simulated.
32 devices in a mesh: head: 8 (over z, y), ctx: 4 (over x, core).
Axes of the slice: x: 2, y: 2, z: 4, core: 2. Of those that a mesh axis runs over, the one named last changes fastest.
Arguments:
- query: bfloat16 [3072, 4096], P(('ctx', 'head')), may hold values from -8 to 8
- key: bfloat16 [3072, 2048], P(('ctx', 'head')), may hold values from -8 to 8
- value: bfloat16 [3072, 2048], P(('ctx', 'head')), may hold values from -8 to 8
- block_order: int32 [8], replicated, may hold values from 0 to 7, each once
Outputs:
- attended: bfloat16 [3072, 4096], P('ctx', 'head')
Inputs may be any that keep to these rules, and one draw needn't show every extreme that they name: `block_order`: each storage block index 0 to 7 appears exactly once.
All inputs are finite; a program needn't handle non-finite values.
Results may differ from a plain program's by a relative error of at most 0.0049.
Values may be sent and summed in bfloat16 or wider, within the bound.
A program may use at most 128 MiB of HBM per device.

v0:
```python
import jax
import jax.numpy as jnp
from jax import lax
from jax.sharding import PartitionSpec as P

HEAD_WIDTH = 128
query_scale = 1.0 / 12.0
softcap_limit = 50.0


def from_behind(value, axis, by):
    size = lax.axis_size(axis)
    return lax.ppermute(value, axis, [(i, (i + by) % size) for i in range(size)])


def block_pos(block_order, which_block, block_len):
    first = lax.dynamic_index_in_dim(block_order, which_block, 0, keepdims=False)
    return first * block_len + lax.iota(jnp.int32, block_len)


def add_block(totals, query_rows, query_pos, key_block, value_block, key_pos):
    numerator, denominator = totals
    scores = (
        jnp.einsum("rhgd,khd->hgrk", query_rows, key_block, preferred_element_type=jnp.float32)
        * query_scale
    )
    capped = softcap_limit * jnp.tanh(scores / softcap_limit)
    visible = key_pos[None, :] <= query_pos[:, None]
    weights = jnp.where(visible[None, None], jnp.exp(capped), jnp.zeros_like(capped))
    denominator = denominator + jnp.sum(weights, axis=-1)
    numerator = numerator + jnp.einsum(
        "hgrk,khd->rhgd",
        weights.astype(jnp.bfloat16),
        value_block,
        preferred_element_type=jnp.float32,
    )
    return (numerator, denominator)


def shards(query, key, value, block_order):
    query, key, value = (
        lax.all_to_all(query, "head", split_axis=1, concat_axis=0, tiled=True),
        lax.all_to_all(key, "head", split_axis=1, concat_axis=0, tiled=True),
        lax.all_to_all(value, "head", split_axis=1, concat_axis=0, tiled=True),
    )
    row_count = query.shape[0]
    block_len = row_count // 2
    kv_heads = key.shape[1] // HEAD_WIDTH
    group_size = query.shape[1] // key.shape[1]
    query_rows = query.reshape(row_count, kv_heads, group_size, HEAD_WIDTH)
    kv_pair = jnp.stack(
        [
            key.reshape(row_count, kv_heads, HEAD_WIDTH),
            value.reshape(row_count, kv_heads, HEAD_WIDTH),
        ]
    )
    cycle_size = lax.axis_size("ctx")
    cycle_index = lax.axis_index("ctx")
    query_pos = jnp.concatenate(
        [
            block_pos(block_order, 2 * cycle_index, block_len),
            block_pos(block_order, 2 * cycle_index + 1, block_len),
        ]
    )
    start_totals = (
        jnp.zeros((row_count, kv_heads, group_size, HEAD_WIDTH), jnp.float32),
        jnp.zeros((kv_heads, group_size, row_count), jnp.float32),
    )

    def add_shard(totals, held, source):
        for which_half in range(2):
            lower = which_half * block_len
            key_pos = block_pos(block_order, 2 * source + which_half, block_len)
            totals = add_block(
                totals,
                query_rows,
                query_pos,
                held[0, lower : lower + block_len],
                held[1, lower : lower + block_len],
                key_pos,
            )
        return totals

    totals = add_shard(start_totals, kv_pair, cycle_index)

    def from_lower(held):
        return from_behind(held, "ctx", 1)

    def turn_both(turn_index, state):
        forward_kv, backward_kv, sums = state
        forward_kv = from_lower(forward_kv)
        backward_kv = from_behind(backward_kv, "ctx", -1)
        sums = add_shard(sums, forward_kv, (cycle_index - turn_index) % cycle_size)
        sums = add_shard(sums, backward_kv, (cycle_index + turn_index) % cycle_size)
        return (forward_kv, backward_kv, sums)

    forward_kv, backward_kv, totals = lax.fori_loop(
        1, cycle_size // 2, turn_both, (kv_pair, kv_pair, totals)
    )
    forward_kv = from_lower(forward_kv)
    totals = add_shard(totals, forward_kv, (cycle_index + cycle_size // 2) % cycle_size)
    numerator, denominator = totals
    result = numerator / jnp.transpose(denominator, (2, 0, 1))[..., None]
    return result.reshape(row_count, kv_heads * group_size * HEAD_WIDTH).astype(jnp.bfloat16)


def solution(mesh):
    placed = (P(("ctx", "head"), None), P(("ctx", "head"), None), P(("ctx", "head"), None), P())
    return jax.shard_map(
        shards, mesh=mesh, in_specs=placed, out_specs=P("ctx", "head"), check_vma=False
    )
```

profile of v0, /device:TPU:1, one launch (start us, length us, event | category | flops | bytes accessed | tf_op | source)
XLA Modules:
  0.0 99.2 jit_solution(4919566508490505928)
XLA Ops:
  1.8 6.4 %all-to-all-start = ((bf16[96,8,256]{2,0,1:T(8,128)(2,1)}), bf16[96,8,256]{2,0,1:T(8,128)(2,1)S(1)}, u32[]{:S(2)}, u32[]{:S(2)}) async-start(bf16[96,8,256]{2,0,1:T(8,128)(2,1)} %bitcast.228), calls=%async_computation | async-start | bytes 786432 | tf_op jit(solution)/shard_map/all_to_all | solution.py:43
  9.9 7.4 %all-to-all-done = bf16[96,8,256]{2,0,1:T(8,128)(2,1)S(1)} async-done(((bf16[96,8,256]{2,0,1:T(8,128)(2,1)}), bf16[96,8,256]{2,0,1:T(8,128)(2,1)S(1)}, u32[]{:S(2)}, u32[]{:S(2)}) %all-to-all-start) | async-done | bytes 393248 | tf_op jit(solution)/shard_map/all_to_all | solution.py:43
  17.3 6.1 %all-to-all-start.2 = ((bf16[96,8,256]{2,0,1:T(8,128)(2,1)}), bf16[96,8,256]{2,0,1:T(8,128)(2,1)S(1)}, u32[]{:S(2)}, u32[]{:S(2)}) async-start(bf16[96,8,256]{2,0,1:T(8,128)(2,1)} %bitcast.229), calls=%async_computation.2 | async-start | bytes 786432 | tf_op jit(solution)/shard_map/all_to_all | solution.py:44
  28.8 2.1 %copy.133 = bf16[12,8,8,512]{3,2,0,1:T(8,128)(2,1)} copy(bf16[12,8,8,512]{3,2,1,0:T(8,128)(2,1)} %bitcast.234) | data formatting | bytes 1572864 | tf_op jit(solution)/shard_map/all_to_all | solution.py:42
  32.5 6.1 %all-to-all-start.1 = ((bf16[96,8,512]{2,0,1:T(8,128)(2,1)}), bf16[96,8,512]{2,0,1:T(8,128)(2,1)S(1)}, u32[]{:S(2)}, u32[]{:S(2)}) async-start(bf16[96,8,512]{2,0,1:T(8,128)(2,1)} %bitcast.227), calls=%async_computation.1 | async-start | bytes 1572864 | tf_op jit(solution)/shard_map/all_to_all | solution.py:42
  39.8 2.4 %broadcast_compare_fusion = (pred[768,384]{0,1:T(8,128)(4,1)S(1)}, pred[768,384]{0,1:T(8,128)(4,1)}, pred[768,384]{0,1:T(8,128)(4,1)S(1)}, pred[768,384]{0,1:T(8...) fusion(s32[768]{0:T(1024)S(1)} %pad_add_fusion, ...), kind=kLoop, calls=%fused_computation.49 | loop fusion | flops 2359296 | bytes 2374656 | tf_op jit(solution)/shard_map/le | solution.py:28
  44.0 2.2 %collective-permute-start = (bf16[2,768,2,128]{3,1,2,0:T(8,128)(2,1)}, bf16[2,768,2,128]{3,1,2,0:T(8,128)(2,1)}, u32[]{:S(2)}, u32[]{:S(2)}) collective-permute-start(bf16[2,768,2,128]{3,1,2,0:T(8,128)(2,1)} %copy_dynamic-update-slice_fusion), channel_id=1, source_target_pairs={{0,1},{1,2},{2,3},{3,0},{4,5},{5,6},{6,7},{7,4},{8,9},{9,10},{10,1... | collective-permute-start | bytes 2359304 | tf_op jit(solution)/shard_map/while/body/eval_jaxpr/ppermute | solution.py:13
  46.9 10.7 %all-to-all-done.1 = bf16[96,8,512]{2,0,1:T(8,128)(2,1)S(1)} async-done(((bf16[96,8,512]{2,0,1:T(8,128)(2,1)}), bf16[96,8,512]{2,0,1:T(8,128)(2,1)S(1)}, u32[]{:S(2)}, u32[]{:S(2)}) %all-to-all-start.1) | async-done | bytes 786464 | tf_op jit(solution)/shard_map/all_to_all | solution.py:42
  57.8 2.8 %fusion = (f32[2,2,768]{2,1,0:T(2,128)S(1)}, f32[2,384,768,2]{2,1,3,0:T(8,128)S(1)}) fusion(pred[768,384]{0,1:T(8,128)(4,1)} %get-tuple-element.46, bf16[768,2,2,128]{3,2,1,0:T(2,128)(2,1)S(1)} %reshape.260, bf16[1,768,2,128]{3,1,2,0:T(8,128)(2,1)S(1)} %get-tuple-element.25), kind=kOutput, calls=%fused_computation.8 | convolution fusion | flops 306705408 | bytes 6008832 | tf_op jit(solution)/shard_map/rhgd,khd->hgrk/dot_general | solution.py:24
  60.6 1.8 %fusion.30 = f32[2,2,768,128]{2,3,1,0:T(8,128)S(1)} fusion(f32[2,384,768,2]{2,1,3,0:T(8,128)S(1)} %get-tuple-element.68, pred[768,384]{0,1:T(8,128)(4,1)S(1)} %copy-done.3, bf16[1,384,2,128]{1,3,2,0:T(8,128)(2,1)S(1)} %copy.90), kind=kOutput, calls=%fused_computation.31 | convolution fusion | flops 306708480 | bytes 6782976 | tf_op jit(solution)/shard_map/hgrk,khd->rhgd/dot_general | solution.py:31
  62.4 1.8 %fusion.2 = (f32[2,2,768]{2,1,0:T(2,128)S(1)}, f32[2,384,768,2]{2,1,3,0:T(8,128)S(1)}) fusion(pred[768,384]{0,1:T(8,128)(4,1)S(1)} %copy-done.2, bf16[768,2,2,128]{3,2,1,0:T(2,128)(2,1)S(1)} %reshape.260, bf16[1,768,2,128]{3,1,2,0:T(8,128)(2,1)S(1)} %get-tuple-element.25), kind=kOutput, calls=%fused_computation.10 | convolution fusion | flops 306705408 | bytes 6008832 | tf_op jit(solution)/shard_map/rhgd,khd->hgrk/dot_general | solution.py:24
  64.2 1.8 %fusion.28 = f32[2,2,768,128]{2,3,1,0:T(8,128)S(1)} fusion(f32[2,384,768,2]{2,1,3,0:T(8,128)S(1)} %get-tuple-element.70, pred[768,384]{0,1:T(8,128)(4,1)S(1)} %copy-done.2, bf16[1,384,2,128]{1,3,2,0:T(8,128)(2,1)S(1)} %copy.91), kind=kOutput, calls=%fused_computation.30 | convolution fusion | flops 306708480 | bytes 6782976 | tf_op jit(solution)/shard_map/hgrk,khd->rhgd/dot_general | solution.py:31
  66.0 3.5 %collective-permute-start.2 = (bf16[2,768,2,128]{3,1,2,0:T(8,128)(2,1)}, bf16[2,768,2,128]{3,1,2,0:T(8,128)(2,1)S(1)}, u32[]{:S(2)}, u32[]{:S(2)}) collective-permute-start(bf16[2,768,2,128]{3,1,2,0:T(8,128)(2,1)} %collective-permute-done), channel_id=1, source_target_pairs={{0,1},{1,2},{2,3},{3,0},{4,5},{5,6},{6,7},{7,4},{8,9},{9,10},{10,1... | collective-permute-start | bytes 2359304 | tf_op jit(solution)/shard_map/ppermute | solution.py:13
  69.5 2.7 %fusion.10 = (f32[2,2,768]{2,1,0:T(2,128)S(1)}, f32[2,384,768,2]{2,1,3,0:T(8,128)S(1)}) fusion(pred[768,384]{0,1:T(8,128)(4,1)S(1)} %copy-done.1, bf16[768,2,2,128]{3,2,1,0:T(2,128)(2,1)S(1)} %reshape.260, bf16[2,768,2,128]{3,1,2,0:T(8,128)(2,1)} %collective-permute-done.1), kind=kOutput, calls=%fused_computation.18 | convolution fusion | flops 306705408 | bytes 6008832 | tf_op jit(solution)/shard_map/while/body/eval_jaxpr/rhgd,khd->hgrk/dot_general | solution.py:24
  72.2 2.6 %fusion.20 = f32[2,128,2,768]{3,1,2,0:T(8,128)S(1)} fusion(f32[2,384,768,2]{2,1,3,0:T(8,128)S(1)} %get-tuple-element.60, pred[768,384]{0,1:T(8,128)(4,1)S(1)} %copy-done.1, bf16[2,768,2,128]{3,1,2,0:T(8,128)(2,1)} %collective-permute-done.1), kind=kOutput, calls=%fused_computation.26 | convolution fusion | flops 306708480 | bytes 6782976 | tf_op jit(solution)/shard_map/while/body/eval_jaxpr/hgrk,khd->rhgd/dot_general | solution.py:31
  74.8 2.7 %fusion.8 = (f32[2,2,768]{2,1,0:T(2,128)S(1)}, f32[2,384,768,2]{2,1,3,0:T(8,128)S(1)}) fusion(pred[768,384]{0,1:T(8,128)(4,1)S(1)} %copy-done, bf16[768,2,2,128]{3,2,1,0:T(2,128)(2,1)S(1)} %reshape.260, bf16[2,768,2,128]{3,1,2,0:T(8,128)(2,1)} %collective-permute-done.1), kind=kOutput, calls=%fused_computation.16 | convolution fusion | flops 306705408 | bytes 6008832 | tf_op jit(solution)/shard_map/while/body/eval_jaxpr/rhgd,khd->hgrk/dot_general | solution.py:24
  77.5 2.5 %fusion.22 = f32[2,128,2,768]{3,1,2,0:T(8,128)S(1)} fusion(f32[2,384,768,2]{2,1,3,0:T(8,128)S(1)} %get-tuple-element.62, pred[768,384]{0,1:T(8,128)(4,1)S(1)} %copy-done, bf16[2,768,2,128]{3,1,2,0:T(8,128)(2,1)} %collective-permute-done.1), kind=kOutput, calls=%fused_computation.27 | convolution fusion | flops 306708480 | bytes 6782976 | tf_op jit(solution)/shard_map/while/body/eval_jaxpr/hgrk,khd->rhgd/dot_general | solution.py:31
  80.1 2.7 %fusion.6 = (f32[2,2,768]{2,1,0:T(2,128)S(1)}, f32[2,384,768,2]{2,1,3,0:T(8,128)S(1)}) fusion(pred[768,384]{0,1:T(8,128)(4,1)S(1)} %get-tuple-element.40, bf16[768,2,2,128]{3,2,1,0:T(2,128)(2,1)S(1)} %reshape.260, bf16[2,768,2,128]{3,1,2,0:T(8,128)(2,1)} %collective-permute-done), kind=kOutput, calls=%fused_computation.14 | convolution fusion | flops 306705408 | bytes 6008832 | tf_op jit(solution)/shard_map/while/body/eval_jaxpr/rhgd,khd->hgrk/dot_general | solution.py:24
  82.8 2.5 %fusion.24 = f32[2,128,2,768]{3,1,2,0:T(8,128)S(1)} fusion(f32[2,384,768,2]{2,1,3,0:T(8,128)S(1)} %get-tuple-element.64, pred[768,384]{0,1:T(8,128)(4,1)S(1)} %get-tuple-element.40, bf16[2,768,2,128]{3,1,2,0:T(8,128)(2,1)} %collective-permute-done), kind=kOutput, calls=%fused_computation.28 | convolution fusion | flops 306708480 | bytes 6782976 | tf_op jit(solution)/shard_map/while/body/eval_jaxpr/hgrk,khd->rhgd/dot_general | solution.py:31
  85.3 2.7 %fusion.4 = (f32[2,2,768]{2,1,0:T(2,128)S(1)}, f32[2,384,768,2]{2,1,3,0:T(8,128)S(1)}) fusion(pred[768,384]{0,1:T(8,128)(4,1)S(1)} %get-tuple-element.29, bf16[768,2,2,128]{3,2,1,0:T(2,128)(2,1)S(1)} %reshape.260, bf16[2,768,2,128]{3,1,2,0:T(8,128)(2,1)} %collective-permute-done), kind=kOutput, calls=%fused_computation.12 | convolution fusion | flops 306705408 | bytes 6008832 | tf_op jit(solution)/shard_map/while/body/eval_jaxpr/rhgd,khd->hgrk/dot_general | solution.py:24
  88.1 2.7 %fusion.26 = f32[2,128,2,768]{3,1,2,0:T(8,128)S(1)} fusion(f32[2,384,768,2]{2,1,3,0:T(8,128)S(1)} %get-tuple-element.66, pred[768,384]{0,1:T(8,128)(4,1)S(1)} %get-tuple-element.29, bf16[2,768,2,128]{3,1,2,0:T(8,128)(2,1)} %collective-permute-done), kind=kOutput, calls=%fused_computation.29 | convolution fusion | flops 306708480 | bytes 6782976 | tf_op jit(solution)/shard_map/while/body/eval_jaxpr/hgrk,khd->rhgd/dot_general | solution.py:31
  90.8 1.8 %fusion.12 = (f32[2,2,768]{2,1,0:T(2,128)S(1)}, f32[2,384,768,2]{2,1,3,0:T(8,128)S(1)}) fusion(pred[768,384]{0,1:T(8,128)(4,1)S(1)} %get-tuple-element.45, bf16[768,2,2,128]{3,2,1,0:T(2,128)(2,1)S(1)} %reshape.260, bf16[2,768,2,128]{3,1,2,0:T(8,128)(2,1)S(1)} %collective-permute-done.2), kind=kOutput, calls=%fused_computation.20 | convolution fusion | flops 306705408 | bytes 6008832 | tf_op jit(solution)/shard_map/rhgd,khd->hgrk/dot_general | solution.py:24
  92.6 1.8 %fusion.14 = (f32[2,2,768]{2,1,0:T(2,128)S(1)}, f32[2,384,768,2]{2,1,3,0:T(8,128)S(1)}) fusion(pred[768,384]{0,1:T(8,128)(4,1)S(1)} %get-tuple-element.27, bf16[768,2,2,128]{3,2,1,0:T(2,128)(2,1)S(1)} %reshape.260, bf16[2,768,2,128]{3,1,2,0:T(8,128)(2,1)S(1)} %collective-permute-done.2), kind=kOutput, calls=%fused_computation.22 | convolution fusion | flops 306705408 | bytes 6008832 | tf_op jit(solution)/shard_map/rhgd,khd->hgrk/dot_general | solution.py:24
  96.1 2.0 %fusion.41 = bf16[768,2,2,128]{0,3,2,1:T(8,128)(2,1)S(1)} fusion(f32[2,128,2,768]{3,1,2,0:T(8,128)S(1)} %fusion.18, f32[2,128,2,768]{3,1,2,0:T(8,128)S(1)} %fusion.20, f32[2,128,2,768]{3,1,2,0:T(8,128)S(1)} %fusion.22, f32[2,128,2,768]{3,1,2,0:T(8,128)S(1)} %fusion.24, f32[2,128,2,768]{3,1,2,0:T(8,128)S(1)} %fusion.26, f32[2,2,768,128]{2,3,1,0:T(8,128)S(1)} %fusion.30, ...), kind=kOutput, calls=%fused_computation.42 | convolution fusion | flops 310247424 | bytes 17018880 | tf_op jit(solution)/shard_map/hgrk,khd->rhgd/dot_general | solution.py:31
  (32 shorter events, 12.3 us)
Async XLA Ops:
  1.8 15.5 %all-to-all-start = ((bf16[96,8,256]{2,0,1:T(8,128)(2,1)}), bf16[96,8,256]{2,0,1:T(8,128)(2,1)S(1)}, u32[]{:S(2)}, u32[]{:S(2)}) async-start(bf16[96,8,256]{2,0,1:T(8,128)(2,1)} %bitcast.228), calls=%async_computation | async-start | bytes 786432 | tf_op jit(solution)/shard_map/all_to_all | solution.py:43
  17.3 15.2 %all-to-all-start.2 = ((bf16[96,8,256]{2,0,1:T(8,128)(2,1)}), bf16[96,8,256]{2,0,1:T(8,128)(2,1)S(1)}, u32[]{:S(2)}, u32[]{:S(2)}) async-start(bf16[96,8,256]{2,0,1:T(8,128)(2,1)} %bitcast.229), calls=%async_computation.2 | async-start | bytes 786432 | tf_op jit(solution)/shard_map/all_to_all | solution.py:44
  32.5 25.1 %all-to-all-start.1 = ((bf16[96,8,512]{2,0,1:T(8,128)(2,1)}), bf16[96,8,512]{2,0,1:T(8,128)(2,1)S(1)}, u32[]{:S(2)}, u32[]{:S(2)}) async-start(bf16[96,8,512]{2,0,1:T(8,128)(2,1)} %bitcast.227), calls=%async_computation.1 | async-start | bytes 1572864 | tf_op jit(solution)/shard_map/all_to_all | solution.py:42
  44.0 22.0 %collective-permute-start = (bf16[2,768,2,128]{3,1,2,0:T(8,128)(2,1)}, bf16[2,768,2,128]{3,1,2,0:T(8,128)(2,1)}, u32[]{:S(2)}, u32[]{:S(2)}) collective-permute-start(bf16[2,768,2,128]{3,1,2,0:T(8,128)(2,1)} %copy_dynamic-update-slice_fusion), channel_id=1, source_target_pairs={{0,1},{1,2},{2,3},{3,0},{4,5},{5,6},{6,7},{7,4},{8,9},{9,10},{10,1... | collective-permute-start | bytes 2359304 | tf_op jit(solution)/shard_map/while/body/eval_jaxpr/ppermute | solution.py:13
  46.3 23.2 %collective-permute-start.1 = (bf16[2,768,2,128]{3,1,2,0:T(8,128)(2,1)}, bf16[2,768,2,128]{3,1,2,0:T(8,128)(2,1)}, u32[]{:S(2)}, u32[]{:S(2)}) collective-permute-start(bf16[2,768,2,128]{3,1,2,0:T(8,128)(2,1)} %copy_dynamic-update-slice_fusion), channel_id=1, source_target_pairs={{0,3},{1,0},{2,1},{3,2},{4,7},{5,4},{6,5},{7,6},{8,11},{9,8},{10,9... | collective-permute-start | bytes 2359304 | tf_op jit(solution)/shard_map/while/body/eval_jaxpr/ppermute | solution.py:13
  57.8 2.8 %copy-start.3 = (pred[768,384]{0,1:T(8,128)(4,1)S(1)}, pred[768,384]{0,1:T(8,128)(4,1)}, u32[]{:S(2)}) copy-start(pred[768,384]{0,1:T(8,128)(4,1)} %get-tuple-element.46) | copy-start | bytes 884740
  60.6 1.8 %copy-start.2 = (pred[768,384]{0,1:T(8,128)(4,1)S(1)}, pred[768,384]{0,1:T(8,128)(4,1)}, u32[]{:S(2)}) copy-start(pred[768,384]{0,1:T(8,128)(4,1)} %get-tuple-element.28) | copy-start | bytes 884740
  64.2 5.3 %copy-start.1 = (pred[768,384]{0,1:T(8,128)(4,1)S(1)}, pred[768,384]{0,1:T(8,128)(4,1)}, u32[]{:S(2)}) copy-start(pred[768,384]{0,1:T(8,128)(4,1)} %get-tuple-element.44) | copy-start | bytes 884740
  66.0 24.8 %collective-permute-start.2 = (bf16[2,768,2,128]{3,1,2,0:T(8,128)(2,1)}, bf16[2,768,2,128]{3,1,2,0:T(8,128)(2,1)S(1)}, u32[]{:S(2)}, u32[]{:S(2)}) collective-permute-start(bf16[2,768,2,128]{3,1,2,0:T(8,128)(2,1)} %collective-permute-done), channel_id=1, source_target_pairs={{0,1},{1,2},{2,3},{3,0},{4,5},{5,6},{6,7},{7,4},{8,9},{9,10},{10,1... | collective-permute-start | bytes 2359304 | tf_op jit(solution)/shard_map/ppermute | solution.py:13
  72.2 2.6 %copy-start = (pred[768,384]{0,1:T(8,128)(4,1)S(1)}, pred[768,384]{0,1:T(8,128)(4,1)}, u32[]{:S(2)}) copy-start(pred[768,384]{0,1:T(8,128)(4,1)} %get-tuple-element.42) | copy-start | bytes 884740
where the time goes:
time: 100 us; the launch traced here: 99.2 us
  matrix products  36.6 us (37%)
  starting transfers between devices  24.2 us (24%)
  waiting for transfers between devices  19.7 us (20%)
  local copies, waits for them, and re-layouts  11.1 us (11%)
  between operations  5.27 us (5%)
  other arithmetic  2.43 us (2%)
    dot_general x8, matrix products, add_block(): jnp.einsum('rhgd,khd->hgrk', query_rows, key_block, preferred_element_typ...  19 us
    dot_general x8, matrix products, add_block(): jnp.einsum('hgrk,khd->rhgd', weights.astype(jnp.bfloat16), value_block, p...  17.6 us
    all_to_all x1, waiting for transfers between devices, shards(): lax.all_to_all(query, 'head', split_axis=1, concat_axis=0, tiled=True)  10.7 us
    all_to_all x1, waiting for transfers between devices, shards(): lax.all_to_all(key, 'head', split_axis=1, concat_axis=0, tiled=True)  7.41 us
    all_to_all x1, starting transfers between devices, shards(): lax.all_to_all(key, 'head', split_axis=1, concat_axis=0, tiled=True)  6.37 us
    all_to_all x1, starting transfers between devices, shards(): lax.all_to_all(query, 'head', split_axis=1, concat_axis=0, tiled=True)  6.06 us
    all_to_all x1, starting transfers between devices, shards(): lax.all_to_all(value, 'head', split_axis=1, concat_axis=0, tiled=True)  6.06 us
    ppermute x3, starting transfers between devices, from_behind(): lax.ppermute(value, axis, [(i, (i + by) % size) for i in range(size)])  5.67 us
  transfers between devices with their start and end apart: 6, of which 3 were waited for; matrix products, arithmetic and copies ran while one was open for 40% of the time, Pallas kernels for 0%

commit v1 on v0

--- a/solution.py
+++ b/solution.py
@@ -6,6 +6,13 @@
 HEAD_WIDTH = 128
 query_scale = 1.0 / 12.0
 softcap_limit = 50.0
+
+
+def swap_blocks(shard, axis, split, join):
+    n_dev = lax.axis_size(axis)
+    pieces = jnp.stack(jnp.split(shard, n_dev, axis=split), axis=0)
+    pieces = lax.all_to_all(pieces, axis, split_axis=0, concat_axis=0)
+    return jnp.concatenate(pieces, axis=join)
 
 
 def from_behind(value, axis, by):
@@ -41,7 +48,7 @@
     query, key, value = (
         lax.all_to_all(query, "head", split_axis=1, concat_axis=0, tiled=True),
         lax.all_to_all(key, "head", split_axis=1, concat_axis=0, tiled=True),
-        lax.all_to_all(value, "head", split_axis=1, concat_axis=0, tiled=True),
+        swap_blocks(value, "head", 1, 0),
     )
     row_count = query.shape[0]
     block_len = row_count // 2

time: 100 us -> 102 us (1.020)
  local copies, waits for them, and re-layouts: 11.1 us -> 20.7 us
  waiting for transfers between devices: 19.7 us -> 12.2 us
    unnamed x10 -> x17, local copies, waits for them, and re-layouts: 0.37 us -> 10.3 us
    all_to_all x1, waiting for transfers between devices: 7.41 us -> 0.01 us  [shards(): lax.all_to_all(key, 'head', split_axis=1, concat_axis=0, tiled=True)]
    all_to_all x1 -> x0, local copies, waits for them, and re-layouts: 1.76 us -> none  [shards(): lax.all_to_all(value, 'head', split_axis=1, concat_axis=0, tiled=True)]
    another operation x0 -> x1, local copies, waits for them, and re-layouts: none -> 1.41 us  [swap_blocks(): pieces = jnp.stack(jnp.split(shard, n_dev, axis=split), axis=0)]
  transfers between devices with their start and end apart: 6 -> 6, of which waited for: 3 -> 2; matrix products, arithmetic and copies ran while one was open for 40% -> 49% of each run, Pallas kernels for 0% -> 0%
where the time goes in v1:
time: 102 us; the launch traced here: 101 us
  matrix products  36.6 us (36%)
  starting transfers between devices  23.6 us (23%)
  local copies, waits for them, and re-layouts  20.7 us (20%)
  waiting for transfers between devices  12.2 us (12%)
  between operations  5.27 us (5%)
  other arithmetic  2.43 us (2%)
    dot_general x8, matrix products, add_block(): jnp.einsum('rhgd,khd->hgrk', query_rows, key_block, preferred_element_typ...  19 us
    dot_general x8, matrix products, add_block(): jnp.einsum('hgrk,khd->rhgd', weights.astype(jnp.bfloat16), value_block, p...  17.6 us
    all_to_all x1, waiting for transfers between devices, shards(): lax.all_to_all(query, 'head', split_axis=1, concat_axis=0, tiled=True)  10.6 us
    unnamed x17, local copies, waits for them, and re-layouts  10.3 us
    all_to_all x1, starting transfers between devices, shards(): lax.all_to_all(key, 'head', split_axis=1, concat_axis=0, tiled=True)  6.37 us
    all_to_all x1, starting transfers between devices, shards(): lax.all_to_all(query, 'head', split_axis=1, concat_axis=0, tiled=True)  6.02 us
    ppermute x3, starting transfers between devices, from_behind(): lax.ppermute(value, axis, [(i, (i + by) % size) for i in range(size)])  5.77 us
    all_to_all x1, starting transfers between devices, swap_blocks(): pieces = lax.all_to_all(pieces, axis, split_axis=0, concat_axis=0)  5.44 us
  transfers between devices with their start and end apart: 6, of which 2 were waited for; matrix products, arithmetic and copies ran while one was open for 49% of the time, Pallas kernels for 0%

profile of v1, /device:TPU:1, one launch (start us, length us, event | category | flops | bytes accessed | tf_op | source)
XLA Modules:
  0.0 100.8 jit_solution(12166987249404651843)
XLA Ops:
  0.0 1.8 %copy.131 = bf16[12,8,8,256]{3,2,0,1:T(8,128)(2,1)} copy(bf16[12,8,8,256]{3,2,1,0:T(8,128)(2,1)} %bitcast.223) | data formatting | bytes 786432 | tf_op jit(solution)/shard_map/all_to_all | solution.py:50
  1.8 6.4 %all-to-all-start.1 = ((bf16[96,8,256]{2,0,1:T(8,128)(2,1)}), bf16[96,8,256]{2,0,1:T(8,128)(2,1)S(1)}, u32[]{:S(2)}, u32[]{:S(2)}) async-start(bf16[96,8,256]{2,0,1:T(8,128)(2,1)} %bitcast.218), calls=%async_computation.1 | async-start | bytes 786432 | tf_op jit(solution)/shard_map/all_to_all | solution.py:50
  19.5 5.4 %all-to-all-start = ((bf16[8,96,256]{2,1,0:T(8,128)(2,1)}), bf16[8,96,256]{2,1,0:T(8,128)(2,1)S(1)}, u32[]{:S(2)}, u32[]{:S(2)}) async-start(bf16[8,96,256]{2,1,0:T(8,128)(2,1)} %bitcast_dynamic-update-slice_fusion), calls=%async_computation | async-start | bytes 786432 | tf_op jit(solution)/shard_map/all_to_all | solution.py:14
  30.3 2.1 %copy.130 = bf16[12,8,8,512]{3,2,0,1:T(8,128)(2,1)} copy(bf16[12,8,8,512]{3,2,1,0:T(8,128)(2,1)} %bitcast.222) | data formatting | bytes 1572864 | tf_op jit(solution)/shard_map/all_to_all | solution.py:49
  34.0 6.0 %all-to-all-start.2 = ((bf16[96,8,512]{2,0,1:T(8,128)(2,1)}), bf16[96,8,512]{2,0,1:T(8,128)(2,1)S(1)}, u32[]{:S(2)}, u32[]{:S(2)}) async-start(bf16[96,8,512]{2,0,1:T(8,128)(2,1)} %bitcast.217), calls=%async_computation.2 | async-start | bytes 1572864 | tf_op jit(solution)/shard_map/all_to_all | solution.py:49
  41.3 2.4 %broadcast_compare_fusion = (pred[768,384]{0,1:T(8,128)(4,1)S(1)}, pred[768,384]{0,1:T(8,128)(4,1)}, pred[768,384]{0,1:T(8,128)(4,1)S(1)}, pred[768,384]{0,1:T(8...) fusion(s32[768]{0:T(1024)S(1)} %pad_add_fusion, ...), kind=kLoop, calls=%fused_computation.43 | loop fusion | flops 2359296 | bytes 2374656 | tf_op jit(solution)/shard_map/le | solution.py:35
  45.6 2.3 %collective-permute-start = (bf16[2,768,2,128]{3,1,2,0:T(8,128)(2,1)}, bf16[2,768,2,128]{3,1,2,0:T(8,128)(2,1)}, u32[]{:S(2)}, u32[]{:S(2)}) collective-permute-start(bf16[2,768,2,128]{3,1,2,0:T(8,128)(2,1)} %copy_dynamic-update-slice_fusion), channel_id=1, source_target_pairs={{0,1},{1,2},{2,3},{3,0},{4,5},{5,6},{6,7},{7,4},{8,9},{9,10},{10,1... | collective-permute-start | bytes 2359304 | tf_op jit(solution)/shard_map/while/body/eval_jaxpr/ppermute | solution.py:20
  48.5 10.6 %all-to-all-done.2 = bf16[96,8,512]{2,0,1:T(8,128)(2,1)S(1)} async-done(((bf16[96,8,512]{2,0,1:T(8,128)(2,1)}), bf16[96,8,512]{2,0,1:T(8,128)(2,1)S(1)}, u32[]{:S(2)}, u32[]{:S(2)}) %all-to-all-start.2) | async-done | bytes 786464 | tf_op jit(solution)/shard_map/all_to_all | solution.py:49
  59.3 2.8 %fusion = (f32[2,2,768]{2,1,0:T(2,128)S(1)}, f32[2,384,768,2]{2,1,3,0:T(8,128)S(1)}) fusion(pred[768,384]{0,1:T(8,128)(4,1)} %get-tuple-element.46, bf16[768,2,2,128]{3,2,1,0:T(2,128)(2,1)S(1)} %reshape.256, bf16[1,768,2,128]{3,1,2,0:T(8,128)(2,1)S(1)} %get-tuple-element.25), kind=kOutput, calls=%fused_computation.8 | convolution fusion | flops 306705408 | bytes 6008832 | tf_op jit(solution)/shard_map/rhgd,khd->hgrk/dot_general | solution.py:31
  62.1 1.8 %fusion.30 = f32[2,128,2,768]{3,1,2,0:T(8,128)S(1)} fusion(f32[2,384,768,2]{2,1,3,0:T(8,128)S(1)} %get-tuple-element.68, pred[768,384]{0,1:T(8,128)(4,1)S(1)} %copy-done.3, bf16[1,384,2,128]{1,3,2,0:T(8,128)(2,1)S(1)} %copy.89), kind=kOutput, calls=%fused_computation.31 | convolution fusion | flops 306708480 | bytes 6782976 | tf_op jit(solution)/shard_map/hgrk,khd->rhgd/dot_general | solution.py:38
  63.9 1.8 %fusion.2 = (f32[2,2,768]{2,1,0:T(2,128)S(1)}, f32[2,384,768,2]{2,1,3,0:T(8,128)S(1)}) fusion(pred[768,384]{0,1:T(8,128)(4,1)S(1)} %copy-done.2, bf16[768,2,2,128]{3,2,1,0:T(2,128)(2,1)S(1)} %reshape.256, bf16[1,768,2,128]{3,1,2,0:T(8,128)(2,1)S(1)} %get-tuple-element.25), kind=kOutput, calls=%fused_computation.10 | convolution fusion | flops 306705408 | bytes 6008832 | tf_op jit(solution)/shard_map/rhgd,khd->hgrk/dot_general | solution.py:31
  65.7 1.8 %fusion.28 = f32[2,128,2,768]{3,1,2,0:T(8,128)S(1)} fusion(f32[2,384,768,2]{2,1,3,0:T(8,128)S(1)} %get-tuple-element.70, pred[768,384]{0,1:T(8,128)(4,1)S(1)} %copy-done.2, bf16[1,384,2,128]{1,3,2,0:T(8,128)(2,1)S(1)} %copy.90), kind=kOutput, calls=%fused_computation.30 | convolution fusion | flops 306708480 | bytes 6782976 | tf_op jit(solution)/shard_map/hgrk,khd->rhgd/dot_general | solution.py:38
  67.5 3.5 %collective-permute-start.2 = (bf16[2,768,2,128]{3,1,2,0:T(8,128)(2,1)}, bf16[2,768,2,128]{3,1,2,0:T(8,128)(2,1)S(1)}, u32[]{:S(2)}, u32[]{:S(2)}) collective-permute-start(bf16[2,768,2,128]{3,1,2,0:T(8,128)(2,1)} %collective-permute-done), channel_id=1, source_target_pairs={{0,1},{1,2},{2,3},{3,0},{4,5},{5,6},{6,7},{7,4},{8,9},{9,10},{10,1... | collective-permute-start | bytes 2359304 | tf_op jit(solution)/shard_map/ppermute | solution.py:20
  71.0 2.7 %fusion.10 = (f32[2,2,768]{2,1,0:T(2,128)S(1)}, f32[2,384,768,2]{2,1,3,0:T(8,128)S(1)}) fusion(pred[768,384]{0,1:T(8,128)(4,1)S(1)} %copy-done.1, bf16[768,2,2,128]{3,2,1,0:T(2,128)(2,1)S(1)} %reshape.256, bf16[2,768,2,128]{3,1,2,0:T(8,128)(2,1)} %collective-permute-done.1), kind=kOutput, calls=%fused_computation.18 | convolution fusion | flops 306705408 | bytes 6008832 | tf_op jit(solution)/shard_map/while/body/eval_jaxpr/rhgd,khd->hgrk/dot_general | solution.py:31
  73.7 2.6 %fusion.20 = f32[2,128,2,768]{3,1,2,0:T(8,128)S(1)} fusion(f32[2,384,768,2]{2,1,3,0:T(8,128)S(1)} %get-tuple-element.60, pred[768,384]{0,1:T(8,128)(4,1)S(1)} %copy-done.1, bf16[2,768,2,128]{3,1,2,0:T(8,128)(2,1)} %collective-permute-done.1), kind=kOutput, calls=%fused_computation.26 | convolution fusion | flops 306708480 | bytes 6782976 | tf_op jit(solution)/shard_map/while/body/eval_jaxpr/hgrk,khd->rhgd/dot_general | solution.py:38
  76.3 2.7 %fusion.8 = (f32[2,2,768]{2,1,0:T(2,128)S(1)}, f32[2,384,768,2]{2,1,3,0:T(8,128)S(1)}) fusion(pred[768,384]{0,1:T(8,128)(4,1)S(1)} %copy-done, bf16[768,2,2,128]{3,2,1,0:T(2,128)(2,1)S(1)} %reshape.256, bf16[2,768,2,128]{3,1,2,0:T(8,128)(2,1)} %collective-permute-done.1), kind=kOutput, calls=%fused_computation.16 | convolution fusion | flops 306705408 | bytes 6008832 | tf_op jit(solution)/shard_map/while/body/eval_jaxpr/rhgd,khd->hgrk/dot_general | solution.py:31
  79.1 2.5 %fusion.22 = f32[2,128,2,768]{3,1,2,0:T(8,128)S(1)} fusion(f32[2,384,768,2]{2,1,3,0:T(8,128)S(1)} %get-tuple-element.62, pred[768,384]{0,1:T(8,128)(4,1)S(1)} %copy-done, bf16[2,768,2,128]{3,1,2,0:T(8,128)(2,1)} %collective-permute-done.1), kind=kOutput, calls=%fused_computation.27 | convolution fusion | flops 306708480 | bytes 6782976 | tf_op jit(solution)/shard_map/while/body/eval_jaxpr/hgrk,khd->rhgd/dot_general | solution.py:38
  81.6 2.7 %fusion.6 = (f32[2,2,768]{2,1,0:T(2,128)S(1)}, f32[2,384,768,2]{2,1,3,0:T(8,128)S(1)}) fusion(pred[768,384]{0,1:T(8,128)(4,1)S(1)} %get-tuple-element.40, bf16[768,2,2,128]{3,2,1,0:T(2,128)(2,1)S(1)} %reshape.256, bf16[2,768,2,128]{3,1,2,0:T(8,128)(2,1)} %collective-permute-done), kind=kOutput, calls=%fused_computation.14 | convolution fusion | flops 306705408 | bytes 6008832 | tf_op jit(solution)/shard_map/while/body/eval_jaxpr/rhgd,khd->hgrk/dot_general | solution.py:31
  84.3 2.5 %fusion.24 = f32[2,128,2,768]{3,1,2,0:T(8,128)S(1)} fusion(f32[2,384,768,2]{2,1,3,0:T(8,128)S(1)} %get-tuple-element.64, pred[768,384]{0,1:T(8,128)(4,1)S(1)} %get-tuple-element.40, bf16[2,768,2,128]{3,1,2,0:T(8,128)(2,1)} %collective-permute-done), kind=kOutput, calls=%fused_computation.28 | convolution fusion | flops 306708480 | bytes 6782976 | tf_op jit(solution)/shard_map/while/body/eval_jaxpr/hgrk,khd->rhgd/dot_general | solution.py:38
  86.9 2.7 %fusion.4 = (f32[2,2,768]{2,1,0:T(2,128)S(1)}, f32[2,384,768,2]{2,1,3,0:T(8,128)S(1)}) fusion(pred[768,384]{0,1:T(8,128)(4,1)S(1)} %get-tuple-element.29, bf16[768,2,2,128]{3,2,1,0:T(2,128)(2,1)S(1)} %reshape.256, bf16[2,768,2,128]{3,1,2,0:T(8,128)(2,1)} %collective-permute-done), kind=kOutput, calls=%fused_computation.12 | convolution fusion | flops 306705408 | bytes 6008832 | tf_op jit(solution)/shard_map/while/body/eval_jaxpr/rhgd,khd->hgrk/dot_general | solution.py:31
  89.6 2.7 %fusion.26 = f32[2,128,2,768]{3,1,2,0:T(8,128)S(1)} fusion(f32[2,384,768,2]{2,1,3,0:T(8,128)S(1)} %get-tuple-element.66, pred[768,384]{0,1:T(8,128)(4,1)S(1)} %get-tuple-element.29, bf16[2,768,2,128]{3,1,2,0:T(8,128)(2,1)} %collective-permute-done), kind=kOutput, calls=%fused_computation.29 | convolution fusion | flops 306708480 | bytes 6782976 | tf_op jit(solution)/shard_map/while/body/eval_jaxpr/hgrk,khd->rhgd/dot_general | solution.py:38
  92.3 1.8 %fusion.12 = (f32[2,2,768]{2,1,0:T(2,128)S(1)}, f32[2,384,768,2]{2,1,3,0:T(8,128)S(1)}) fusion(pred[768,384]{0,1:T(8,128)(4,1)S(1)} %get-tuple-element.45, bf16[768,2,2,128]{3,2,1,0:T(2,128)(2,1)S(1)} %reshape.256, bf16[2,768,2,128]{3,1,2,0:T(8,128)(2,1)S(1)} %collective-permute-done.2), kind=kOutput, calls=%fused_computation.20 | convolution fusion | flops 306705408 | bytes 6008832 | tf_op jit(solution)/shard_map/rhgd,khd->hgrk/dot_general | solution.py:31
  94.1 1.8 %fusion.14 = (f32[2,2,768]{2,1,0:T(2,128)S(1)}, f32[2,384,768,2]{2,1,3,0:T(8,128)S(1)}) fusion(pred[768,384]{0,1:T(8,128)(4,1)S(1)} %get-tuple-element.27, bf16[768,2,2,128]{3,2,1,0:T(2,128)(2,1)S(1)} %reshape.256, bf16[2,768,2,128]{3,1,2,0:T(8,128)(2,1)S(1)} %collective-permute-done.2), kind=kOutput, calls=%fused_computation.22 | convolution fusion | flops 306705408 | bytes 6008832 | tf_op jit(solution)/shard_map/rhgd,khd->hgrk/dot_general | solution.py:31
  97.6 2.0 %fusion.40 = bf16[768,2,2,128]{0,3,2,1:T(8,128)(2,1)S(1)} fusion(f32[2,128,2,768]{3,1,2,0:T(8,128)S(1)} %fusion.18, f32[2,128,2,768]{3,1,2,0:T(8,128)S(1)} %fusion.20, f32[2,128,2,768]{3,1,2,0:T(8,128)S(1)} %fusion.22, f32[2,128,2,768]{3,1,2,0:T(8,128)S(1)} %fusion.24, f32[2,128,2,768]{3,1,2,0:T(8,128)S(1)} %fusion.26, f32[2,128,2,768]{3,1,2,0:T(8,128)S(1)} %fusion.30, ...), kind=kOutput, calls=%fused_computation.41 | convolution fusion | flops 310247424 | bytes 17018880 | tf_op jit(solution)/shard_map/hgrk,khd->rhgd/dot_general | solution.py:38
  (39 shorter events, 20.1 us)
Async XLA Ops:
  1.8 17.7 %all-to-all-start.1 = ((bf16[96,8,256]{2,0,1:T(8,128)(2,1)}), bf16[96,8,256]{2,0,1:T(8,128)(2,1)S(1)}, u32[]{:S(2)}, u32[]{:S(2)}) async-start(bf16[96,8,256]{2,0,1:T(8,128)(2,1)} %bitcast.218), calls=%async_computation.1 | async-start | bytes 786432 | tf_op jit(solution)/shard_map/all_to_all | solution.py:50
  19.5 14.6 %all-to-all-start = ((bf16[8,96,256]{2,1,0:T(8,128)(2,1)}), bf16[8,96,256]{2,1,0:T(8,128)(2,1)S(1)}, u32[]{:S(2)}, u32[]{:S(2)}) async-start(bf16[8,96,256]{2,1,0:T(8,128)(2,1)} %bitcast_dynamic-update-slice_fusion), calls=%async_computation | async-start | bytes 786432 | tf_op jit(solution)/shard_map/all_to_all | solution.py:14
  34.0 25.0 %all-to-all-start.2 = ((bf16[96,8,512]{2,0,1:T(8,128)(2,1)}), bf16[96,8,512]{2,0,1:T(8,128)(2,1)S(1)}, u32[]{:S(2)}, u32[]{:S(2)}) async-start(bf16[96,8,512]{2,0,1:T(8,128)(2,1)} %bitcast.217), calls=%async_computation.2 | async-start | bytes 1572864 | tf_op jit(solution)/shard_map/all_to_all | solution.py:49
  45.6 21.9 %collective-permute-start = (bf16[2,768,2,128]{3,1,2,0:T(8,128)(2,1)}, bf16[2,768,2,128]{3,1,2,0:T(8,128)(2,1)}, u32[]{:S(2)}, u32[]{:S(2)}) collective-permute-start(bf16[2,768,2,128]{3,1,2,0:T(8,128)(2,1)} %copy_dynamic-update-slice_fusion), channel_id=1, source_target_pairs={{0,1},{1,2},{2,3},{3,0},{4,5},{5,6},{6,7},{7,4},{8,9},{9,10},{10,1... | collective-permute-start | bytes 2359304 | tf_op jit(solution)/shard_map/while/body/eval_jaxpr/ppermute | solution.py:20
  47.8 23.2 %collective-permute-start.1 = (bf16[2,768,2,128]{3,1,2,0:T(8,128)(2,1)}, bf16[2,768,2,128]{3,1,2,0:T(8,128)(2,1)}, u32[]{:S(2)}, u32[]{:S(2)}) collective-permute-start(bf16[2,768,2,128]{3,1,2,0:T(8,128)(2,1)} %copy_dynamic-update-slice_fusion), channel_id=1, source_target_pairs={{0,3},{1,0},{2,1},{3,2},{4,7},{5,4},{6,5},{7,6},{8,11},{9,8},{10,9... | collective-permute-start | bytes 2359304 | tf_op jit(solution)/shard_map/while/body/eval_jaxpr/ppermute | solution.py:20
  59.3 2.8 %copy-start.3 = (pred[768,384]{0,1:T(8,128)(4,1)S(1)}, pred[768,384]{0,1:T(8,128)(4,1)}, u32[]{:S(2)}) copy-start(pred[768,384]{0,1:T(8,128)(4,1)} %get-tuple-element.46) | copy-start | bytes 884740
  62.1 1.8 %copy-start.2 = (pred[768,384]{0,1:T(8,128)(4,1)S(1)}, pred[768,384]{0,1:T(8,128)(4,1)}, u32[]{:S(2)}) copy-start(pred[768,384]{0,1:T(8,128)(4,1)} %get-tuple-element.28) | copy-start | bytes 884740
  65.7 5.3 %copy-start.1 = (pred[768,384]{0,1:T(8,128)(4,1)S(1)}, pred[768,384]{0,1:T(8,128)(4,1)}, u32[]{:S(2)}) copy-start(pred[768,384]{0,1:T(8,128)(4,1)} %get-tuple-element.44) | copy-start | bytes 884740
  67.5 24.8 %collective-permute-start.2 = (bf16[2,768,2,128]{3,1,2,0:T(8,128)(2,1)}, bf16[2,768,2,128]{3,1,2,0:T(8,128)(2,1)S(1)}, u32[]{:S(2)}, u32[]{:S(2)}) collective-permute-start(bf16[2,768,2,128]{3,1,2,0:T(8,128)(2,1)} %collective-permute-done), channel_id=1, source_target_pairs={{0,1},{1,2},{2,3},{3,0},{4,5},{5,6},{6,7},{7,4},{8,9},{9,10},{10,1... | collective-permute-start | bytes 2359304 | tf_op jit(solution)/shard_map/ppermute | solution.py:20
  73.7 2.6 %copy-start = (pred[768,384]{0,1:T(8,128)(4,1)S(1)}, pred[768,384]{0,1:T(8,128)(4,1)}, u32[]{:S(2)}) copy-start(pred[768,384]{0,1:T(8,128)(4,1)} %get-tuple-element.42) | copy-start | bytes 884740
